TPU v7x, 256 devices: a whole 4x4x8 slice. The times are simulated.
256 devices in a mesh: tp: 4 (over x), dp: 64 (over z, y, core).
Axes of the slice: x: 4, y: 4, z: 8, core: 2. Of those that a mesh axis runs over, the one named last changes fastest.
Arguments:
- item_query: bfloat16 [8192, 2048], P('dp', 'tp'), may hold values from -20 to 20, as said below
- item_keys: bfloat16 [8192, 4, 2048], P('dp', None, 'tp'), may hold values from -20 to 20
- item_values: bfloat16 [8192, 4, 2048], P('dp', None, 'tp'), may hold values from -6 to 6
- item_out_weight: bfloat16 [2048, 4096], P('tp'), may hold values from -0.125 to 0.125
- item_residual: bfloat16 [8192, 4096], P('dp'), may hold values from -3 to 3
- cite_home: int32 [65536, 1], P('dp'), may hold values from 0 to 63; in each aligned block of 1024 rows (0 to 1023, 1024 to 2047, ...) at most 24 rows name the same one
- cite_row: int32 [65536], P('dp'), may hold values from 0 to 127
- seq_length: int32 [64], P('dp'), may hold values from 1 to 1024, 40960 in all
- user_gain: float32 [4096], replicated, may hold values from 0.1 to 1.9
- user_weight: bfloat16 [4096, 16, 384], P('dp', 'tp'), may hold values from -0.09375 to 0.09375
Outputs:
- user_qkv: bfloat16 [65536, 16, 384], P('dp', 'tp')
Inputs may be any that keep to these rules, and one draw needn't show every extreme that they name: `item_query`: in hidden draws some items' queries equal a multiple of keys at their last two tokens. `cite_home`: among the 1024 positions of one sequence at most 24 cite items of one home device, and some home device is cited exactly 24 times. `seq_length`: some sequence has all 1024 positions live.
All inputs are finite; a program needn't handle non-finite values. No bound on the sum of `seq_length` on one device may be relied on, other than what follows from the above.
Results may differ from a plain program's by a relative error of at most 0.0065.
Values may be sent and summed in bfloat16 or wider, within the bound.
No kernel may reach another device: no remote copies, remote signals or barrier semaphores. Data moves between devices by JAX's collectives and lax.ppermute only.
A program may use at most 128 MiB of HBM per device.

v0:
```python
import math
import jax
import jax.numpy as jnp
from jax import lax
from jax.sharding import PartitionSpec as P

HEAD_DIM = 128


def cut_along(x, dim, size):
    before, after = (x.shape[:dim], x.shape[dim + 1 :])
    return jnp.moveaxis(x.reshape(*before, size, -1, *after), dim, 0)


def sent_and_summed(x, axis, dim):
    parts = cut_along(x, dim, lax.axis_size(axis))
    arrived = lax.all_to_all(parts, axis, split_axis=0, concat_axis=0, tiled=True)
    return arrived.sum(axis=0)


def per_device(
    item_query,
    item_keys,
    item_values,
    item_out_weight,
    item_residual,
    cite_home,
    cite_row,
    seq_length,
    user_gain,
    user_weight,
):
    count_items, width_heads = item_query.shape
    tokens_item = item_keys.shape[1]
    local_heads = width_heads // HEAD_DIM
    queries = item_query.reshape(count_items, local_heads, HEAD_DIM)
    keys_all = item_keys.reshape(count_items, tokens_item, local_heads, HEAD_DIM)
    values_all = item_values.reshape(count_items, tokens_item, local_heads, HEAD_DIM)
    scores = jnp.einsum("ihd,ithd->iht", queries, keys_all, preferred_element_type=jnp.float32) * (
        1.0 / math.sqrt(HEAD_DIM)
    )
    probs = jax.nn.softmax(scores, axis=-1).astype(jnp.bfloat16)
    attended = jnp.einsum("iht,ithd->ihd", probs, values_all, preferred_element_type=jnp.float32)
    attended = attended.astype(jnp.bfloat16).reshape(count_items, width_heads)
    partial_value = jnp.dot(attended, item_out_weight, preferred_element_type=jnp.float32)
    summed = sent_and_summed(partial_value, "tp", 1)
    columns = summed.shape[1]
    own_cols = lax.dynamic_slice_in_dim(item_residual, lax.axis_index("tp") * columns, columns, 1)
    item_vec = (summed + own_cols.astype(jnp.float32)).astype(jnp.bfloat16)
    home_dev = cite_home[:, 0]
    length_seq = home_dev.shape[0]
    devices = lax.axis_size("dp")
    capacity = 3 * length_seq // (2 * devices)
    onehot = (home_dev[:, None] == jnp.arange(devices, dtype=jnp.int32)[None, :]).astype(jnp.int32)
    before = jnp.cumsum(onehot, axis=0) - onehot
    slot_index = jnp.sum(before * onehot, axis=1)
    target = home_dev * capacity + slot_index
    wanted = (
        jnp.zeros((devices * capacity,), jnp.int32)
        .at[target]
        .set(cite_row)
        .reshape(devices, capacity)
    )
    asked = lax.all_to_all(wanted, "dp", split_axis=0, concat_axis=0, tiled=True)
    looked = jnp.take(item_vec, asked.reshape(-1), axis=0).reshape(
        devices, capacity, item_vec.shape[1]
    )
    answers = lax.all_to_all(looked, "dp", split_axis=0, concat_axis=0, tiled=True)
    cited = jnp.take(answers.reshape(devices * capacity, item_vec.shape[1]), target, axis=0)
    cited = lax.all_gather(cited, "tp", axis=1, tiled=True)
    values32 = cited.astype(jnp.float32)
    scale = lax.rsqrt(jnp.mean(values32 * values32, axis=1, keepdims=True) + 1e-05)
    normed = (values32 * scale * user_gain[None, :]).astype(jnp.bfloat16)
    shard_rows, user_heads, triple = user_weight.shape
    weight_flat = user_weight.reshape(shard_rows, user_heads * triple)
    projected = jnp.dot(
        normed,
        lax.all_gather(weight_flat, "dp", axis=0, tiled=True),
        preferred_element_type=jnp.float32,
    )
    live = jnp.arange(length_seq, dtype=jnp.int32) < seq_length[0]
    masked = jnp.where(live[:, None], projected, jnp.zeros_like(projected))
    return masked.astype(jnp.bfloat16).reshape(length_seq, user_heads, triple)


def solution(mesh):
    in_specs = (
        P("dp", "tp"),
        P("dp", None, "tp"),
        P("dp", None, "tp"),
        P("tp", None),
        P("dp", None),
        P("dp", None),
        P("dp"),
        P("dp"),
        P(),
        P("dp", "tp", None),
    )
    out_specs = P("dp", "tp", None)
    return jax.shard_map(
        per_device, mesh=mesh, in_specs=in_specs, out_specs=out_specs, check_vma=False
    )
```

profile of v0, /device:TPU:1, one launch (start us, length us, event | category | flops | bytes accessed | tf_op | source)
XLA Modules:
  0.0 401.7 jit_solution(5603883770292417331)
XLA Ops:
  6.5 0.8 fusion.23
  7.3 18.0 %reduce-window.6 = s32[64,8,128]{2,1,0:T(8,128)S(1)} reduce-window(s32[64,8,128]{2,1,0:T(8,128)S(1)} %fusion.23, s32[]{:T(128)} %constant.20.clone.1), window={size=1x1x128 pad=0_0x0_0x127_0}, to_apply=%region_0.0 | reduce-window | flops 8323072 | bytes 524292 | tf_op jit(solution)/shard_map/reduce-window
  25.9 0.8 fusion.22
  26.6 0.7 and_reduce_fusion
  27.4 4.5 %scatter_custom_fusion = s32[1536]{0:T(1024)S(1)} fusion(s32[1024]{0:T(1024)S(1)} %bitcast.69, s32[1024]{0:T(1024)} %param.16, s32[]{:T(128)} %constant.20.clone.1), kind=kCustom, calls=%fused_computation.46 | custom fusion | bytes 6656 | tf_op jit(solution)/shard_map/scatter | solution.py:61
  31.8 0.7 all_to_all.12
  32.5 13.1 %all-to-all-start = ((s32[64,1,24]{2,1,0:T(1,128)}), s32[64,1,24]{2,1,0:T(1,128)S(1)}, u32[]{:S(2)}, u32[]{:S(2)}) async-start(s32[64,1,24]{2,1,0:T(1,128)} %bitcast.7), calls=%async_computation | async-start | bytes 65536 | tf_op jit(solution)/shard_map/all_to_all | solution.py:64
  45.7 1.3 reshape.152
  47.0 1.7 fusion.18
  48.9 0.2 copy.26
  49.1 0.7 fusion.16
  49.9 6.5 %copy.29 = bf16[4096,512]{1,0:T(8,128)(2,1)} copy(bf16[4096,512]{0,1:T(8,128)(2,1)} %bitcast.59) | data formatting | bytes 8388608 | tf_op jit(solution)/shard_map/dot_general | solution.py:45
  56.4 5.0 %convolution_bitcast_fusion = f32[4,128,1024]{2,1,0:T(8,128)} fusion(bf16[128,512,1]{1,0,2:T(8,128)(2,1)S(1)} %reshape.150, bf16[4,1024,512]{2,1,0:T(8,128)(2,1)} %bitcast.57), kind=kOutput, calls=%fused_computation.16 | convolution fusion | flops 536870912 | bytes 6422528 | tf_op jit(solution)/shard_map/dot_general | solution.py:45
  61.3 4.0 %all-to-all-start.1 = ((f32[4,128,1024]{2,1,0:T(8,128)}), f32[4,128,1024]{2,1,0:T(8,128)S(1)}, u32[]{:S(2)}, u32[]{:S(2)}) async-start(f32[4,128,1024]{2,1,0:T(8,128)} %convolution_bitcast_fusion), calls=%async_computation.1 | async-start | bytes 4194304 | tf_op jit(solution)/shard_map/all_to_all | solution.py:17
  65.4 0.6 broadcast.90
  66.0 0.8 reduce.7
  66.9 24.2 %all-to-all-done.1 = f32[4,128,1024]{2,1,0:T(8,128)S(1)} async-done(((f32[4,128,1024]{2,1,0:T(8,128)}), f32[4,128,1024]{2,1,0:T(8,128)S(1)}, u32[]{:S(2)}, u32[]{:S(2)}) %all-to-all-start.1) | async-done | bytes 2097184 | tf_op jit(solution)/shard_map/all_to_all | solution.py:17
  91.1 0.2 reduce_sum.41
  91.3 1.0 add_convert_fusion
  92.3 5.8 %gather_fusion = bf16[1536,1024]{1,0:T(8,128)(2,1)} fusion(bf16[128,1024]{1,0:T(8,128)(2,1)S(1)} %add_convert_fusion, s32[2048]{0:T(1024)S(1)} %pad_clamp_fusion), kind=kCustom, calls=%fused_computation | custom fusion | bytes 6297600 | tf_op jit(solution)/shard_map/jit(_take)/gather | solution.py:65
  98.1 3.3 broadcast_select_fusion
  101.3 11.7 %all-to-all-start.2 = ((bf16[64,24,1024]{2,1,0:T(8,128)(2,1)}), bf16[64,24,1024]{2,1,0:T(8,128)(2,1)}, u32[]{:S(2)}, u32[]{:S(2)}) async-start(bf16[64,24,1024]{2,1,0:T(8,128)(2,1)} %broadcast_select_fusion), calls=%async_computation.2 | async-start | bytes 6291456 | tf_op jit(solution)/shard_map/all_to_all | solution.py:68
  113.1 72.3 %all-to-all-done.2 = bf16[64,24,1024]{2,1,0:T(8,128)(2,1)} async-done(((bf16[64,24,1024]{2,1,0:T(8,128)(2,1)}), bf16[64,24,1024]{2,1,0:T(8,128)(2,1)}, u32[]{:S(2)}, u32[]{:S(2)}) %all-to-all-start.2) | async-done | bytes 3145760 | tf_op jit(solution)/shard_map/all_to_all | solution.py:68
  185.4 7.3 %gather_fusion.1 = bf16[1024,1024]{1,0:T(8,128)(2,1)S(1)} fusion(bf16[1536,1024]{1,0:T(8,128)(2,1)} %bitcast.19, s32[1024]{0:T(1024)S(1)} %broadcast_clamp_fusion), kind=kCustom, calls=%fused_computation.1 | custom fusion | bytes 4198400 | tf_op jit(solution)/shard_map/jit(_take)/gather | solution.py:69
  192.7 1.6 broadcast_select_fusion.1
  194.3 0.2 all-gather.5.cloned.1.call-start
  194.5 0.7 copy.31
  195.9 79.5 %all-gather.3.cloned.1.call-done = bf16[1024,4096]{1,0:T(8,128)(2,1)} async-done(((bf16[1024,1024]{1,0:T(8,128)(2,1)}), bf16[1024,4096]{1,0:T(8,128)(2,1)}) %all-gather.3.cloned.1.call-update) | async-done | bytes 8388624 | tf_op jit(solution)/shard_map/all_gather | solution.py:70
  275.4 5.1 %fusion.2 = f32[1024]{0:T(1024)S(1)} fusion(bf16[1024,4096]{1,0:T(8,128)(2,1)} %all-gather.3.cloned.1.call-done), kind=kLoop, calls=%fused_computation.7 | loop fusion | flops 12581888 | bytes 8392704 | tf_op jit(solution)/shard_map/reduce_sum | solution.py:72
  280.5 88.8 %all-gather.5.cloned.1.call-done = bf16[4096,1536]{1,0:T(8,128)(2,1)} async-done(((bf16[64,1536]{1,0:T(8,128)(2,1)}), bf16[4096,1536]{1,0:T(8,128)(2,1)}) %all-gather.5.cloned.1.call-update) | async-done | bytes 12582928 | tf_op jit(solution)/shard_map/all_gather | solution.py:78
  369.3 19.3 %select_convert_fusion = bf16[1024,1536]{1,0:T(8,128)(2,1)} fusion(bf16[4096,1536]{1,0:T(8,128)(2,1)} %all-gather.5.cloned.1.call-done, bf16[1024,4096]{1,0:T(8,128)(2,1)} %all-gather.3.cloned.1.call-done, f32[4096]{0:T(1024)S(1)} %copy-done.2, f32[1024]{0:T(1024)S(1)} %add_rsqrt_fusion, pred[1024]{0:T(1024)(128)(4,1)S(1)} %iota_compare_fusion.2), kind=kOutput, calls=%fused_computation.13 | convolution fusion | flops 12904824832 | bytes 24138752 | tf_op jit(solution)/shard_map/dot_general | solution.py:76
  388.6 6.2 %reshape.121 = bf16[1024,4,384]{2,1,0:T(4,128)(2,1)} reshape(bf16[1024,1536]{1,0:T(8,128)(2,1)} %select_convert_fusion) | data formatting | bytes 6291456 | tf_op jit(solution)/shard_map/reshape | solution.py:83
  (27 shorter events, 1.0 us)
Async XLA Ops:
  6.5 42.5 %copy-start = (bf16[128,4,512]{2,1,0:T(4,128)(2,1)S(1)}, bf16[128,4,512]{2,1,0:T(4,128)(2,1)}, u32[]{:S(2)}) copy-start(bf16[128,4,512]{2,1,0:T(4,128)(2,1)} %param.12) | copy-start | bytes 1572868
  32.5 28.8 %all-to-all-start = ((s32[64,1,24]{2,1,0:T(1,128)}), s32[64,1,24]{2,1,0:T(1,128)S(1)}, u32[]{:S(2)}, u32[]{:S(2)}) async-start(s32[64,1,24]{2,1,0:T(1,128)} %bitcast.7), calls=%async_computation | async-start | bytes 65536 | tf_op jit(solution)/shard_map/all_to_all | solution.py:64
  61.3 29.7 %all-to-all-start.1 = ((f32[4,128,1024]{2,1,0:T(8,128)}), f32[4,128,1024]{2,1,0:T(8,128)S(1)}, u32[]{:S(2)}, u32[]{:S(2)}) async-start(f32[4,128,1024]{2,1,0:T(8,128)} %convolution_bitcast_fusion), calls=%async_computation.1 | async-start | bytes 4194304 | tf_op jit(solution)/shard_map/all_to_all | solution.py:17
  101.3 84.0 %all-to-all-start.2 = ((bf16[64,24,1024]{2,1,0:T(8,128)(2,1)}), bf16[64,24,1024]{2,1,0:T(8,128)(2,1)}, u32[]{:S(2)}, u32[]{:S(2)}) async-start(bf16[64,24,1024]{2,1,0:T(8,128)(2,1)} %broadcast_select_fusion), calls=%async_computation.2 | async-start | bytes 6291456 | tf_op jit(solution)/shard_map/all_to_all | solution.py:68
  113.0 162.4 %all-gather.3.cloned.1.call-start = ((), (), s32[]{:S(2)}) async-start(), calls=%async_computation.3 | async-start | bytes 10485760 | tf_op jit(solution)/shard_map/all_gather | solution.py:70
  192.7 1.9 copy-start.1
  194.3 175.0 %all-gather.5.cloned.1.call-start = ((), (), s32[]{:S(2)}) async-start(), calls=%async_computation.4 | async-start | bytes 12779520 | tf_op jit(solution)/shard_map/all_gather | solution.py:78
  195.9 173.3 %copy-start.2 = (f32[4096]{0:T(1024)S(1)}, f32[4096]{0:T(1024)}, u32[]{:S(2)}) copy-start(f32[4096]{0:T(1024)} %param.18) | copy-start | bytes 49156
Sparse Core Ops, SparseCore 0:
  194.4 80.9 all-gather.2
  278.1 91.0 all-gather.4
where the time goes:
time: 403 us; the launch traced here: 402 us
  waiting for transfers between devices  265 us (66%)
  local copies, waits for them, and re-layouts  34.3 us (9%)
  other arithmetic  32.5 us (8%)
  starting transfers between devices  29.1 us (7%)
  matrix products  26.7 us (7%)
  between operations  14.3 us (4%)
    all_gather x1, waiting for transfers between devices, per_device(): lax.all_gather(weight_flat, 'dp', axis=0, tiled=True)  88.8 us
    all_gather x1, waiting for transfers between devices, per_device(): cited = lax.all_gather(cited, 'tp', axis=1, tiled=True)  79.5 us
    all_to_all x1, waiting for transfers between devices, per_device(): lax.all_to_all(looked, 'dp', split_axis=0, concat_axis=0, tiled=True)  72.3 us
    all_to_all x1, waiting for transfers between devices, sent_and_summed(): lax.all_to_all(parts, axis, split_axis=0, concat_axis=0, tiled=True)  24.2 us
    dot_general x1, matrix products, per_device(): jnp.dot(normed, lax.all_gather(weight_flat, 'dp', axis=0, tiled=True), pr...  19.3 us
    another operation x3, other arithmetic  18.2 us
    all_to_all x1, starting transfers between devices, per_device(): lax.all_to_all(wanted, 'dp', split_axis=0, concat_axis=0, tiled=True)  13.1 us
    all_to_all x1, starting transfers between devices, per_device(): lax.all_to_all(looked, 'dp', split_axis=0, concat_axis=0, tiled=True)  11.7 us
  transfers between devices with their start and end apart: 5, of which 4 were waited for; matrix products, arithmetic and copies ran while one was open for 6% of the time, Pallas kernels for 0%

commit v1 on v0

--- a/solution.py
+++ b/solution.py
@@ -5,6 +5,11 @@
 from jax.sharding import PartitionSpec as P
 
 HEAD_DIM = 128
+
+
+def gather_over(x, name, dim):
+    sent = jnp.stack([x] * lax.axis_size(name))
+    return jnp.concatenate(lax.all_to_all(sent, name, 0, 0), axis=dim)
 
 
 def cut_along(x, dim, size):
@@ -74,9 +79,7 @@
     shard_rows, user_heads, triple = user_weight.shape
     weight_flat = user_weight.reshape(shard_rows, user_heads * triple)
     projected = jnp.dot(
-        normed,
-        lax.all_gather(weight_flat, "dp", axis=0, tiled=True),
-        preferred_element_type=jnp.float32,
+        normed, gather_over(weight_flat, "dp", 0), preferred_element_type=jnp.float32
     )
     live = jnp.arange(length_seq, dtype=jnp.int32) < seq_length[0]
     masked = jnp.where(live[:, None], projected, jnp.zeros_like(projected))

time: 403 us -> 506 us (1.26)
  waiting for transfers between devices: 265 us -> 357 us
  starting transfers between devices: 29.1 us -> 36.1 us
    all_to_all x0 -> x1, waiting for transfers between devices: none -> 176 us  [gather_over(): return jnp.concatenate(lax.all_to_all(sent, name, 0, 0), axis=dim)]
    all_gather x1 -> x0, waiting for transfers between devices: 88.8 us -> none  [per_device(): lax.all_gather(weight_flat, 'dp', axis=0, tiled=True)]
    all_to_all x0 -> x1, starting transfers between devices: none -> 7.03 us  [gather_over(): return jnp.concatenate(lax.all_to_all(sent, name, 0, 0), axis=dim)]
    another operation x2 -> x3, local copies, waits for them, and re-layouts: 0.09 us -> 6.08 us  [the longest x1 5.99 us: gather_over(): sent = jnp.stack([x] * lax.axis_size(name))]
where the time goes in v1:
time: 506 us; the launch traced here: 504 us
  waiting for transfers between devices  357 us (71%)
  local copies, waits for them, and re-layouts  37 us (7%)
  starting transfers between devices  36.1 us (7%)
  other arithmetic  32.7 us (6%)
  matrix products  26.8 us (5%)
  between operations  14.3 us (3%)
    all_to_all x1, waiting for transfers between devices, gather_over(): return jnp.concatenate(lax.all_to_all(sent, name, 0, 0), axis=dim)  176 us
    all_gather x1, waiting for transfers between devices, per_device(): cited = lax.all_gather(cited, 'tp', axis=1, tiled=True)  84.1 us
    all_to_all x1, waiting for transfers between devices, per_device(): lax.all_to_all(looked, 'dp', split_axis=0, concat_axis=0, tiled=True)  72.4 us
    all_to_all x1, waiting for transfers between devices, sent_and_summed(): lax.all_to_all(parts, axis, split_axis=0, concat_axis=0, tiled=True)  24.2 us
    dot_general x1, matrix products, per_device(): jnp.dot(normed, gather_over(weight_flat, 'dp', 0), preferred_element_type...  19.4 us
    another operation x3, other arithmetic  18.2 us
    all_to_all x1, starting transfers between devices, per_device(): lax.all_to_all(wanted, 'dp', split_axis=0, concat_axis=0, tiled=True)  13.1 us
    all_to_all x1, starting transfers between devices, per_device(): lax.all_to_all(looked, 'dp', split_axis=0, concat_axis=0, tiled=True)  11.6 us
  transfers between devices with their start and end apart: 5, of which 4 were waited for; matrix products, arithmetic and copies ran while one was open for 6% of the time, Pallas kernels for 0%

profile of v1, /device:TPU:1, one launch (start us, length us, event | category | flops | bytes accessed | tf_op | source)
XLA Modules:
  0.0 503.5 jit_solution(18425990121933258665)
XLA Ops:
  6.5 0.8 fusion.23
  7.3 18.0 %reduce-window.6 = s32[64,8,128]{2,1,0:T(8,128)S(1)} reduce-window(s32[64,8,128]{2,1,0:T(8,128)S(1)} %fusion.23, s32[]{:T(128)} %constant.20.clone.1), window={size=1x1x128 pad=0_0x0_0x127_0}, to_apply=%region_0.0 | reduce-window | flops 8323072 | bytes 524292 | tf_op jit(solution)/shard_map/reduce-window
  25.9 0.8 fusion.22
  26.6 0.7 and_reduce_fusion
  27.4 4.5 scatter_custom_fusion
  31.8 0.7 all_to_all.15
  32.5 13.1 %all-to-all-start = ((s32[64,1,24]{2,1,0:T(1,128)}), s32[64,1,24]{2,1,0:T(1,128)S(1)}, u32[]{:S(2)}, u32[]{:S(2)}) async-start(s32[64,1,24]{2,1,0:T(1,128)} %bitcast.7), calls=%async_computation | async-start | bytes 65536 | tf_op jit(solution)/shard_map/all_to_all | solution.py:69
  45.7 1.3 reshape.154
  47.0 1.7 fusion.18
  48.9 0.2 copy.26
  49.1 0.7 fusion.16
  49.9 6.5 %copy.29 = bf16[4096,512]{1,0:T(8,128)(2,1)} copy(bf16[4096,512]{0,1:T(8,128)(2,1)} %bitcast.60) | data formatting | bytes 8388608 | tf_op jit(solution)/shard_map/dot_general | solution.py:50
  56.4 5.0 convolution_bitcast_fusion
  61.3 4.0 all-to-all-start.1
  65.4 0.6 broadcast.91
  66.0 0.8 reduce.7
  66.9 24.2 %all-to-all-done.1 = f32[4,128,1024]{2,1,0:T(8,128)S(1)} async-done(((f32[4,128,1024]{2,1,0:T(8,128)}), f32[4,128,1024]{2,1,0:T(8,128)S(1)}, u32[]{:S(2)}, u32[]{:S(2)}) %all-to-all-start.1) | async-done | bytes 2097184 | tf_op jit(solution)/shard_map/all_to_all | solution.py:22
  91.3 1.0 add_convert_fusion
  92.3 5.1 %gather_fusion = bf16[1536,1024]{1,0:T(8,128)(2,1)S(1)} fusion(bf16[128,1024]{1,0:T(8,128)(2,1)S(1)} %add_convert_fusion, s32[2048]{0:T(1024)S(1)} %pad_clamp_fusion), kind=kCustom, calls=%fused_computation | custom fusion | bytes 6297600 | tf_op jit(solution)/shard_map/jit(_take)/gather | solution.py:70
  97.4 1.9 broadcast_select_fusion
  99.3 11.6 %all-to-all-start.2 = ((bf16[64,24,1024]{2,1,0:T(8,128)(2,1)}), bf16[64,24,1024]{2,1,0:T(8,128)(2,1)S(1)}, u32[]{:S(2)}, u32[]{:S(2)}) async-start(bf16[64,24,1024]{2,1,0:T(8,128)(2,1)} %broadcast_select_fusion), calls=%async_computation.2 | async-start | bytes 6291456 | tf_op jit(solution)/shard_map/all_to_all | solution.py:73
  110.9 72.4 %all-to-all-done.2 = bf16[64,24,1024]{2,1,0:T(8,128)(2,1)S(1)} async-done(((bf16[64,24,1024]{2,1,0:T(8,128)(2,1)}), bf16[64,24,1024]{2,1,0:T(8,128)(2,1)S(1)}, u32[]{:S(2)}, u32[]{:S(2)}) %all-to-all-start.2) | async-done | bytes 3145760 | tf_op jit(solution)/shard_map/all_to_all | solution.py:73
  183.3 6.0 %stack.3 = bf16[64,64,1536]{2,1,0:T(8,128)(2,1)} broadcast(bf16[64,1536]{1,0:T(8,128)(2,1)S(1)} %bitcast.62), dimensions={1,2} | broadcast | bytes 12779520 | tf_op jit(solution)/shard_map/stack | solution.py:11
  189.3 7.0 %all-to-all-start.3 = ((bf16[64,64,1536]{2,1,0:T(8,128)(2,1)}), bf16[64,64,1536]{2,1,0:T(8,128)(2,1)}, u32[]{:S(2)}, u32[]{:S(2)}) async-start(bf16[64,64,1536]{2,1,0:T(8,128)(2,1)} %stack.3), calls=%async_computation.3 | async-start | bytes 25165824 | tf_op jit(solution)/shard_map/all_to_all | solution.py:12
  196.4 0.2 all-gather.2.cloned.1.call-start
  196.6 5.3 %gather_fusion.1 = bf16[1024,1024]{1,0:T(8,128)(2,1)} fusion(bf16[1536,1024]{1,0:T(8,128)(2,1)S(1)} %bitcast.57, s32[1024]{0:T(1024)S(1)} %broadcast_clamp_fusion), kind=kCustom, calls=%fused_computation.1 | custom fusion | bytes 4198400 | tf_op jit(solution)/shard_map/jit(_take)/gather | solution.py:74
  201.9 3.2 broadcast_select_fusion.1
  205.8 84.1 %all-gather.2.cloned.1.call-done = bf16[1024,4096]{1,0:T(8,128)(2,1)} async-done(((bf16[1024,1024]{1,0:T(8,128)(2,1)}), bf16[1024,4096]{1,0:T(8,128)(2,1)}) %all-gather.2.cloned.1.call-update) | async-done | bytes 8388624 | tf_op jit(solution)/shard_map/all_gather | solution.py:75
  289.9 5.1 %fusion.2 = f32[1024]{0:T(1024)S(1)} fusion(bf16[1024,4096]{1,0:T(8,128)(2,1)} %all-gather.2.cloned.1.call-done), kind=kLoop, calls=%fused_computation.7 | loop fusion | flops 12581888 | bytes 8392704 | tf_op jit(solution)/shard_map/reduce_sum | solution.py:77
  295.0 176.0 %all-to-all-done.3 = bf16[64,64,1536]{2,1,0:T(8,128)(2,1)} async-done(((bf16[64,64,1536]{2,1,0:T(8,128)(2,1)}), bf16[64,64,1536]{2,1,0:T(8,128)(2,1)}, u32[]{:S(2)}, u32[]{:S(2)}) %all-to-all-start.3) | async-done | bytes 12582944 | tf_op jit(solution)/shard_map/all_to_all | solution.py:12
  471.0 19.4 %select_convert_fusion = bf16[1024,1536]{1,0:T(8,128)(2,1)} fusion(bf16[4096,1536]{1,0:T(8,128)(2,1)} %bitcast.20, bf16[1024,4096]{1,0:T(8,128)(2,1)} %all-gather.2.cloned.1.call-done, f32[4096]{0:T(1024)S(1)} %copy-done.3, f32[1024]{0:T(1024)S(1)} %add_rsqrt_fusion, pred[1024]{0:T(1024)(128)(4,1)S(1)} %iota_compare_fusion.2), kind=kOutput, calls=%fused_computation.13 | convolution fusion | flops 12904824832 | bytes 24138752 | tf_op jit(solution)/shard_map/dot_general | solution.py:81
  490.4 6.2 %reshape.123 = bf16[1024,4,384]{2,1,0:T(4,128)(2,1)} reshape(bf16[1024,1536]{1,0:T(8,128)(2,1)} %select_convert_fusion) | data formatting | bytes 6291456 | tf_op jit(solution)/shard_map/reshape | solution.py:86
  (29 shorter events, 1.2 us)
Async XLA Ops:
  6.5 42.5 %copy-start = (bf16[128,4,512]{2,1,0:T(4,128)(2,1)S(1)}, bf16[128,4,512]{2,1,0:T(4,128)(2,1)}, u32[]{:S(2)}) copy-start(bf16[128,4,512]{2,1,0:T(4,128)(2,1)} %param.12) | copy-start | bytes 1572868
  32.5 28.8 %all-to-all-start = ((s32[64,1,24]{2,1,0:T(1,128)}), s32[64,1,24]{2,1,0:T(1,128)S(1)}, u32[]{:S(2)}, u32[]{:S(2)}) async-start(s32[64,1,24]{2,1,0:T(1,128)} %bitcast.7), calls=%async_computation | async-start | bytes 65536 | tf_op jit(solution)/shard_map/all_to_all | solution.py:69
  61.3 29.7 %all-to-all-start.1 = ((f32[4,128,1024]{2,1,0:T(8,128)}), f32[4,128,1024]{2,1,0:T(8,128)S(1)}, u32[]{:S(2)}, u32[]{:S(2)}) async-start(f32[4,128,1024]{2,1,0:T(8,128)} %convolution_bitcast_fusion), calls=%async_computation.1 | async-start | bytes 4194304 | tf_op jit(solution)/shard_map/all_to_all | solution.py:22
  99.3 11.6 %copy-start.2 = (bf16[64,4,384]{2,1,0:T(4,128)(2,1)S(1)}, bf16[64,4,384]{2,1,0:T(4,128)(2,1)}, u32[]{:S(2)}) copy-start(bf16[64,4,384]{2,1,0:T(4,128)(2,1)} %param.19) | copy-start | bytes 589828
  99.3 84.1 %all-to-all-start.2 = ((bf16[64,24,1024]{2,1,0:T(8,128)(2,1)}), bf16[64,24,1024]{2,1,0:T(8,128)(2,1)S(1)}, u32[]{:S(2)}, u32[]{:S(2)}) async-start(bf16[64,24,1024]{2,1,0:T(8,128)(2,1)} %broadcast_select_fusion), calls=%async_computation.2 | async-start | bytes 6291456 | tf_op jit(solution)/shard_map/all_to_all | solution.py:73
  189.3 281.6 %all-to-all-start.3 = ((bf16[64,64,1536]{2,1,0:T(8,128)(2,1)}), bf16[64,64,1536]{2,1,0:T(8,128)(2,1)}, u32[]{:S(2)}, u32[]{:S(2)}) async-start(bf16[64,64,1536]{2,1,0:T(8,128)(2,1)} %stack.3), calls=%async_computation.3 | async-start | bytes 25165824 | tf_op jit(solution)/shard_map/all_to_all | solution.py:12
  196.4 93.6 %all-gather.2.cloned.1.call-start = ((), (), s32[]{:S(2)}) async-start(), calls=%async_computation.4 | async-start | bytes 10485760 | tf_op jit(solution)/shard_map/all_gather | solution.py:75
  205.8 265.2 %copy-start.3 = (f32[4096]{0:T(1024)S(1)}, f32[4096]{0:T(1024)}, u32[]{:S(2)}) copy-start(f32[4096]{0:T(1024)} %param.18) | copy-start | bytes 49156
  471.0 25.7 %copy-start.1 = (bf16[128,4,512]{2,1,0:T(4,128)(2,1)S(1)}, bf16[128,4,512]{2,1,0:T(4,128)(2,1)}, u32[]{:S(2)}) copy-start(bf16[128,4,512]{2,1,0:T(4,128)(2,1)} %param.12) | copy-start | bytes 1572868
Sparse Core Ops, SparseCore 0:
  205.3 84.6 all-gather.1
